TPU v7x, 32 devices: a whole 2x2x4 slice. The times are simulated.
32 devices in a mesh: section: 4 (over z), batch: 2 (over x), tile: 4 (over y, core).
Axes of the slice: x: 2, y: 2, z: 4, core: 2. Of those that a mesh axis runs over, the one named last changes fastest.
Arguments:
- latents: bfloat16 [8, 4, 32, 1280], P('batch', 'tile'), parts along dimension 0, may hold values from -6 to 6
- prompt_tokens: bfloat16 [8, 77, 2048], P('batch'), parts along dimension 0, may hold values from -6 to 6
- fresh_noise: bfloat16 [1, 8, 4, 32, 1280], P(None, 'batch', 'tile'), parts along dimension 1, may hold values from -6 to 6
- timesteps: int32 [2], replicated, may hold values from 600 to 999
- entry_order: int32 [8], P('batch'), parts along dimension 0, may hold values from 0 to 3, each once
- timestep_weight: bfloat16 [4, 320, 1280], P('section'), may hold values from -0.3125 to 0.3125
- conv_kernel: float32 [4, 9, 1280], P('section'), may hold values from -1 to 1
- norm_gain: float32 [4, 1280], P('section'), may hold values from 0.25 to 1.75
- layer_norm_bias: float32 [4, 1280], P('section'), may hold values from -1.5 to 1.5
- qkv_weight: bfloat16 [4, 1280, 3, 1280], P('section', None, None, 'tile'), may hold values from -0.15625 to 0.15625
- prompt_weight: bfloat16 [4, 2048, 2, 1280], P('section', None, None, 'tile'), may hold values from -0.125 to 0.125
- out_weight: bfloat16 [4, 1280, 1280], P('section', 'tile'), may hold values from -0.15625 to 0.15625
Outputs:
- samples: bfloat16 [8, 4, 32, 1280], P('batch', 'tile', None, 'section'), parts along dimension 0
There are 2 independent parts, one for each index of `batch`. A program takes and returns all parts, laid end to end along the dimension named above; an argument that names none is the same for every part. Nothing has to cross between parts.
All inputs are finite; a program needn't handle non-finite values.
Results may differ from a plain program's by a relative error of at most 0.019.
Values may be sent and summed in bfloat16 or wider, within the bound.
A program may use at most 64 MiB of HBM per device.

v0:
```python
import math

import jax
import jax.numpy as jnp
from jax import lax
from jax.sharding import PartitionSpec as P

HEADS = 20


def extended(cells, sides, width):
    for axis, dim in sides:
        count = lax.axis_size(axis)
        ends = count - 1
        head = lax.slice_in_dim(cells, 0, width, axis=dim)
        tail = lax.slice_in_dim(cells, cells.shape[dim] - width, cells.shape[dim], axis=dim)
        cells = jnp.concatenate(
            [
                lax.ppermute(tail, axis, [(i, (i + 1) % count) for i in range(ends)]),
                cells,
                lax.ppermute(head, axis, [((i + 1) % count, i) for i in range(ends)]),
            ],
            axis=dim,
        )
    return cells


def from_behind(shard, axis, by):
    count = lax.axis_size(axis)
    return lax.ppermute(shard, axis, [(i, (i + by) % count) for i in range(count)])


def spread_2(shard, axis, root):
    mine = lax.axis_index(axis) == root
    return lax.psum(jnp.where(mine, shard, jnp.zeros_like(shard)), axis)


def noise_plan():
    positions = jnp.arange(1000, dtype=jnp.float32)
    low_root = math.sqrt(0.00085)
    high_root = math.sqrt(0.012)
    roots = low_root + (high_root - low_root) * positions / 999.0
    return jnp.exp(jnp.cumsum(jnp.log(1.0 - roots * roots)))


def time_features(timesteps, half_count):
    exponents = jnp.arange(half_count, dtype=jnp.float32) / half_count
    freq_row = jnp.exp(-math.log(10000.0) * exponents)
    angles = timesteps.astype(jnp.float32)[:, None] * freq_row[None, :]
    return jnp.concatenate([jnp.cos(angles), jnp.sin(angles)], axis=1).astype(jnp.bfloat16)


def pick_scalar(alpha_table, position):
    hits = jnp.arange(alpha_table.shape[0], dtype=jnp.int32) == position
    return jnp.sum(jnp.where(hits, alpha_table, jnp.zeros_like(alpha_table)))


def pick_integer(int_table, position):
    hits = jnp.arange(int_table.shape[0], dtype=jnp.int32) == position
    return jnp.sum(jnp.where(hits, int_table, jnp.zeros_like(int_table)))


def mix_positions(rimmed, kernel_body):
    row_total = rimmed.shape[0] - 2
    col_total = rimmed.shape[1]
    framed = jnp.pad(rimmed.astype(jnp.float32), ((0, 0), (1, 1), (0, 0)))
    mixed = rimmed[1:-1].astype(jnp.float32)
    for offset_row in range(3):
        for offset_col in range(3):
            mixed = (
                mixed
                + kernel_body[3 * offset_row + offset_col]
                * framed[offset_row : offset_row + row_total, offset_col : offset_col + col_total]
            )
    return mixed


def layer_norm(values_in, scale_row, shift_row):
    centre = jnp.mean(values_in, axis=-1, keepdims=True)
    spread = jnp.mean(jnp.square(values_in - centre), axis=-1, keepdims=True)
    return (values_in - centre) * lax.rsqrt(spread + 1e-05) * scale_row + shift_row


def attend(queries, keys_all, values_all, head_count):
    query_count = queries.shape[0]
    key_count = keys_all.shape[0]
    head_width = queries.shape[1] // head_count
    query_heads = queries.reshape(query_count, head_count, head_width)
    key_heads = keys_all.reshape(key_count, head_count, head_width)
    value_heads = values_all.reshape(key_count, head_count, head_width)
    scores = jnp.einsum(
        "qhd,khd->hqk", query_heads, key_heads, preferred_element_type=jnp.float32
    ) / math.sqrt(head_width)
    powers = jnp.exp(scores)
    soft_weights = (powers / jnp.sum(powers, axis=-1, keepdims=True)).astype(jnp.bfloat16)
    attended = jnp.einsum(
        "hqk,khd->qhd", soft_weights, value_heads, preferred_element_type=jnp.float32
    )
    return attended.reshape(query_count, head_count * head_width).astype(jnp.bfloat16)


def per_device(
    latents,
    prompt_tokens,
    fresh_noise,
    timesteps,
    entry_order,
    timestep_weight,
    conv_kernel,
    norm_gain,
    layer_norm_bias,
    qkv_weight,
    prompt_weight,
    out_weight,
):
    section_count = lax.axis_size("section")
    tile_count = lax.axis_size("tile")
    section_index = lax.axis_index("section")
    micro_count, rows_here, cols_here, width_all = latents.shape
    token_here = rows_here * cols_here
    chain_total = timesteps.shape[0]
    alpha_table = noise_plan()
    feature_rows = time_features(timesteps, timestep_weight.shape[1] // 2)
    timestep_embedding_all = jnp.dot(
        feature_rows, timestep_weight[0], preferred_element_type=jnp.float32
    )
    kernel_body = conv_kernel[0]
    scale_row = norm_gain[0]
    shift_row = layer_norm_bias[0]
    qkv_local = qkv_weight[0]
    prompt_local = prompt_weight[0]
    out_local = out_weight[0]
    local_heads = HEADS // tile_count
    micro_ids = jnp.arange(micro_count, dtype=jnp.int32)

    def prompt_for(latent_id):
        prompt_row = lax.dynamic_index_in_dim(prompt_tokens, latent_id, 0, False)
        local_pair = jnp.einsum(
            "tc,cjd->tjd", prompt_row, prompt_local, preferred_element_type=jnp.float32
        ).astype(jnp.bfloat16)
        return local_pair

    def lift_and_mix(current, temb_row):
        lifted = (current.astype(jnp.float32) + temb_row).astype(jnp.bfloat16)
        rimmed = extended(lifted, (("tile", 0),), 1)
        mixed = mix_positions(rimmed, kernel_body).reshape(token_here, width_all)
        normed = layer_norm(mixed, scale_row, shift_row).astype(jnp.bfloat16)
        return (mixed, normed)

    def section_heads(current, temb_row, prompt_pair):
        mixed, normed = lift_and_mix(current, temb_row)
        normed_all = lax.all_gather(normed, "tile", axis=0, tiled=True)
        projected = jnp.einsum(
            "tc,cjd->tjd", normed_all, qkv_local, preferred_element_type=jnp.float32
        ).astype(jnp.bfloat16)
        keys_all = jnp.concatenate([projected[:, 1], prompt_pair[:, 0]], axis=0)
        values_all = jnp.concatenate([projected[:, 2], prompt_pair[:, 1]], axis=0)
        attended = attend(projected[:, 0], keys_all, values_all, local_heads)
        update = lax.psum_scatter(
            jnp.dot(attended, out_local, preferred_element_type=jnp.float32).astype(jnp.bfloat16),
            "tile",
            scatter_dimension=0,
            tiled=True,
        ).astype(jnp.float32)
        return (mixed + update).astype(jnp.bfloat16).reshape(rows_here, cols_here, width_all)

    def advance(tick_counter, state_pair):
        carried_state, results = state_pair
        incoming = from_behind(carried_state, "section", 1)
        offset = tick_counter - section_index
        chain_level = jnp.floor_divide(offset, section_count)
        slot_index = offset - chain_level * section_count
        active = (offset >= 0) & (chain_level < chain_total) & (slot_index < micro_count)
        level_clip = jnp.clip(chain_level, 0, chain_total - 1)
        slot_clip = jnp.clip(slot_index, 0, micro_count - 1)
        noise_clip = jnp.clip(chain_level - 1, 0, chain_total - 2)
        latent_id = pick_integer(entry_order, slot_clip)
        starting = lax.dynamic_index_in_dim(latents, latent_id, 0, False)
        noise_slab = lax.dynamic_index_in_dim(
            lax.dynamic_index_in_dim(fresh_noise, noise_clip, 0, False), slot_clip, 0, False
        )
        alpha_bar = pick_scalar(alpha_table, pick_integer(timesteps, level_clip))
        renoised = (
            jnp.sqrt(alpha_bar) * incoming.astype(jnp.float32)
            + jnp.sqrt(1.0 - alpha_bar) * noise_slab.astype(jnp.float32)
        ).astype(jnp.bfloat16)
        first_section = section_index == 0
        current = jnp.where(
            first_section & (chain_level == 0),
            starting,
            jnp.where(first_section, renoised, incoming),
        )
        temb_row = lax.dynamic_index_in_dim(timestep_embedding_all, level_clip, 0, False)
        prompt_pair = prompt_for(latent_id)
        computed = section_heads(current, temb_row, prompt_pair)
        produced = jnp.where(active, computed, jnp.zeros_like(computed))
        finishing = active & (section_index == section_count - 1) & (chain_level == chain_total - 1)
        placing = finishing & (micro_ids == latent_id)
        results = jnp.where(placing[:, None, None, None], produced[None], results)
        return (produced, results)

    tick_total = chain_total * section_count + micro_count - 1
    initial_latent = (
        jnp.zeros((rows_here, cols_here, width_all), jnp.bfloat16),
        jnp.zeros_like(latents),
    )
    final_state = lax.fori_loop(0, tick_total, advance, initial_latent)
    gathered = spread_2(final_state[1], "section", section_count - 1)
    share_width = width_all // section_count
    return lax.dynamic_slice_in_dim(gathered, section_index * share_width, share_width, 3)


def solution(mesh):
    placed = (
        P("batch", "tile", None, None),
        P("batch", None, None),
        P(None, "batch", "tile", None, None),
        P(),
        P("batch"),
        P("section", None, None),
        P("section", None, None),
        P("section", None),
        P("section", None),
        P("section", None, None, "tile"),
        P("section", None, None, "tile"),
        P("section", "tile", None),
    )
    return jax.shard_map(
        per_device,
        mesh=mesh,
        in_specs=placed,
        out_specs=P("batch", "tile", None, "section"),
        check_vma=False,
    )
```

profile of v0, /device:TPU:0, one launch (start us, length us, event | category | flops | bytes accessed | tf_op | source)
XLA Modules:
  0.0 719.2 jit_solution(13876428785944258102)
XLA Ops:
  9.0 3.1 copy.18
  14.4 656.9 %while.18 = (s32[]{:T(128)}, bf16[1,32,1280]{2,1,0:T(8,128)(2,1)}, bf16[4,1,32,1280]{3,2,1,0:T(8,128)(2,1)}, s32[]{:T(128)}, pred[]{:T(512)}, /*index=5*/s32[4]{...) while((s32[]{:T(128)}, bf16[1,32,1280]{2,1,0:T(8,128)(2,1)}, ...), condition=%wide.region_10.11_spmd.clone, body=%wide.region_2.10_spmd.clone.sunk | while | flops 658625344 | bytes 26783188 | solution.py:207
  14.5 3.1 collective-permute-start
  32.6 3.0 collective-permute-start.2
  37.7 8.1 %all_gather.12 = bf16[128,1280]{1,0:T(8,128)(2,1)S(1)} all-gather(bf16[32,1280]{1,0:T(8,128)(2,1)S(1)} %add_convert_fusion.5), channel_id=1, replica_groups=mesh['section'=4,'batch'=2,'tile'=4] {'tile'}, dimensions={0}, use_global_device_ids=true | all-gather | bytes 409600 | tf_op jit(solution)/shard_map/while/body/eval_jaxpr/all_gather | solution.py:152
  52.9 19.9 %reduce-scatter.2.cloned.1.call-done = bf16[32,1280]{1,0:T(8,128)(2,1)} async-done(((bf16[128,1280]{1,0:T(8,128)(2,1)}), bf16[32,1280]{1,0:T(8,128)(2,1)}) %reduce-scatter.2.cloned.1.call-update) | async-done | bytes 81936 | tf_op jit(solution)/shard_map/while/body/eval_jaxpr/reduce_scatter | solution.py:159
  92.7 3.0 collective-permute-start.2
  97.8 7.5 %all_gather.12 = bf16[128,1280]{1,0:T(8,128)(2,1)S(1)} all-gather(bf16[32,1280]{1,0:T(8,128)(2,1)S(1)} %add_convert_fusion.5), channel_id=1, replica_groups=mesh['section'=4,'batch'=2,'tile'=4] {'tile'}, dimensions={0}, use_global_device_ids=true | all-gather | bytes 409600 | tf_op jit(solution)/shard_map/while/body/eval_jaxpr/all_gather | solution.py:152
  112.5 19.8 %reduce-scatter.2.cloned.1.call-done = bf16[32,1280]{1,0:T(8,128)(2,1)} async-done(((bf16[128,1280]{1,0:T(8,128)(2,1)}), bf16[32,1280]{1,0:T(8,128)(2,1)}) %reduce-scatter.2.cloned.1.call-update) | async-done | bytes 81936 | tf_op jit(solution)/shard_map/while/body/eval_jaxpr/reduce_scatter | solution.py:159
  152.3 3.0 collective-permute-start.2
  157.4 7.6 %all_gather.12 = bf16[128,1280]{1,0:T(8,128)(2,1)S(1)} all-gather(bf16[32,1280]{1,0:T(8,128)(2,1)S(1)} %add_convert_fusion.5), channel_id=1, replica_groups=mesh['section'=4,'batch'=2,'tile'=4] {'tile'}, dimensions={0}, use_global_device_ids=true | all-gather | bytes 409600 | tf_op jit(solution)/shard_map/while/body/eval_jaxpr/all_gather | solution.py:152
  172.1 19.8 %reduce-scatter.2.cloned.1.call-done = bf16[32,1280]{1,0:T(8,128)(2,1)} async-done(((bf16[128,1280]{1,0:T(8,128)(2,1)}), bf16[32,1280]{1,0:T(8,128)(2,1)}) %reduce-scatter.2.cloned.1.call-update) | async-done | bytes 81936 | tf_op jit(solution)/shard_map/while/body/eval_jaxpr/reduce_scatter | solution.py:159
  211.8 3.0 collective-permute-start.2
  216.9 7.6 %all_gather.12 = bf16[128,1280]{1,0:T(8,128)(2,1)S(1)} all-gather(bf16[32,1280]{1,0:T(8,128)(2,1)S(1)} %add_convert_fusion.5), channel_id=1, replica_groups=mesh['section'=4,'batch'=2,'tile'=4] {'tile'}, dimensions={0}, use_global_device_ids=true | all-gather | bytes 409600 | tf_op jit(solution)/shard_map/while/body/eval_jaxpr/all_gather | solution.py:152
  231.6 19.8 %reduce-scatter.2.cloned.1.call-done = bf16[32,1280]{1,0:T(8,128)(2,1)} async-done(((bf16[128,1280]{1,0:T(8,128)(2,1)}), bf16[32,1280]{1,0:T(8,128)(2,1)}) %reduce-scatter.2.cloned.1.call-update) | async-done | bytes 81936 | tf_op jit(solution)/shard_map/while/body/eval_jaxpr/reduce_scatter | solution.py:159
  271.3 3.0 collective-permute-start.2
  276.4 7.6 %all_gather.12 = bf16[128,1280]{1,0:T(8,128)(2,1)S(1)} all-gather(bf16[32,1280]{1,0:T(8,128)(2,1)S(1)} %add_convert_fusion.5), channel_id=1, replica_groups=mesh['section'=4,'batch'=2,'tile'=4] {'tile'}, dimensions={0}, use_global_device_ids=true | all-gather | bytes 409600 | tf_op jit(solution)/shard_map/while/body/eval_jaxpr/all_gather | solution.py:152
  291.1 19.8 %reduce-scatter.2.cloned.1.call-done = bf16[32,1280]{1,0:T(8,128)(2,1)} async-done(((bf16[128,1280]{1,0:T(8,128)(2,1)}), bf16[32,1280]{1,0:T(8,128)(2,1)}) %reduce-scatter.2.cloned.1.call-update) | async-done | bytes 81936 | tf_op jit(solution)/shard_map/while/body/eval_jaxpr/reduce_scatter | solution.py:159
  330.8 3.0 collective-permute-start.2
  335.9 7.5 %all_gather.12 = bf16[128,1280]{1,0:T(8,128)(2,1)S(1)} all-gather(bf16[32,1280]{1,0:T(8,128)(2,1)S(1)} %add_convert_fusion.5), channel_id=1, replica_groups=mesh['section'=4,'batch'=2,'tile'=4] {'tile'}, dimensions={0}, use_global_device_ids=true | all-gather | bytes 409600 | tf_op jit(solution)/shard_map/while/body/eval_jaxpr/all_gather | solution.py:152
  350.6 19.8 %reduce-scatter.2.cloned.1.call-done = bf16[32,1280]{1,0:T(8,128)(2,1)} async-done(((bf16[128,1280]{1,0:T(8,128)(2,1)}), bf16[32,1280]{1,0:T(8,128)(2,1)}) %reduce-scatter.2.cloned.1.call-update) | async-done | bytes 81936 | tf_op jit(solution)/shard_map/while/body/eval_jaxpr/reduce_scatter | solution.py:159
  395.4 7.6 %all_gather.12 = bf16[128,1280]{1,0:T(8,128)(2,1)S(1)} all-gather(bf16[32,1280]{1,0:T(8,128)(2,1)S(1)} %add_convert_fusion.5), channel_id=1, replica_groups=mesh['section'=4,'batch'=2,'tile'=4] {'tile'}, dimensions={0}, use_global_device_ids=true | all-gather | bytes 409600 | tf_op jit(solution)/shard_map/while/body/eval_jaxpr/all_gather | solution.py:152
  410.1 19.8 %reduce-scatter.2.cloned.1.call-done = bf16[32,1280]{1,0:T(8,128)(2,1)} async-done(((bf16[128,1280]{1,0:T(8,128)(2,1)}), bf16[32,1280]{1,0:T(8,128)(2,1)}) %reduce-scatter.2.cloned.1.call-update) | async-done | bytes 81936 | tf_op jit(solution)/shard_map/while/body/eval_jaxpr/reduce_scatter | solution.py:159
  455.0 7.5 %all_gather.12 = bf16[128,1280]{1,0:T(8,128)(2,1)S(1)} all-gather(bf16[32,1280]{1,0:T(8,128)(2,1)S(1)} %add_convert_fusion.5), channel_id=1, replica_groups=mesh['section'=4,'batch'=2,'tile'=4] {'tile'}, dimensions={0}, use_global_device_ids=true | all-gather | bytes 409600 | tf_op jit(solution)/shard_map/while/body/eval_jaxpr/all_gather | solution.py:152
  469.6 19.8 %reduce-scatter.2.cloned.1.call-done = bf16[32,1280]{1,0:T(8,128)(2,1)} async-done(((bf16[128,1280]{1,0:T(8,128)(2,1)}), bf16[32,1280]{1,0:T(8,128)(2,1)}) %reduce-scatter.2.cloned.1.call-update) | async-done | bytes 81936 | tf_op jit(solution)/shard_map/while/body/eval_jaxpr/reduce_scatter | solution.py:159
  514.5 7.5 %all_gather.12 = bf16[128,1280]{1,0:T(8,128)(2,1)S(1)} all-gather(bf16[32,1280]{1,0:T(8,128)(2,1)S(1)} %add_convert_fusion.5), channel_id=1, replica_groups=mesh['section'=4,'batch'=2,'tile'=4] {'tile'}, dimensions={0}, use_global_device_ids=true | all-gather | bytes 409600 | tf_op jit(solution)/shard_map/while/body/eval_jaxpr/all_gather | solution.py:152
  529.1 19.8 %reduce-scatter.2.cloned.1.call-done = bf16[32,1280]{1,0:T(8,128)(2,1)} async-done(((bf16[128,1280]{1,0:T(8,128)(2,1)}), bf16[32,1280]{1,0:T(8,128)(2,1)}) %reduce-scatter.2.cloned.1.call-update) | async-done | bytes 81936 | tf_op jit(solution)/shard_map/while/body/eval_jaxpr/reduce_scatter | solution.py:159
  574.0 7.5 %all_gather.12 = bf16[128,1280]{1,0:T(8,128)(2,1)S(1)} all-gather(bf16[32,1280]{1,0:T(8,128)(2,1)S(1)} %add_convert_fusion.5), channel_id=1, replica_groups=mesh['section'=4,'batch'=2,'tile'=4] {'tile'}, dimensions={0}, use_global_device_ids=true | all-gather | bytes 409600 | tf_op jit(solution)/shard_map/while/body/eval_jaxpr/all_gather | solution.py:152
  588.6 19.8 %reduce-scatter.2.cloned.1.call-done = bf16[32,1280]{1,0:T(8,128)(2,1)} async-done(((bf16[128,1280]{1,0:T(8,128)(2,1)}), bf16[32,1280]{1,0:T(8,128)(2,1)}) %reduce-scatter.2.cloned.1.call-update) | async-done | bytes 81936 | tf_op jit(solution)/shard_map/while/body/eval_jaxpr/reduce_scatter | solution.py:159
  633.5 7.5 %all_gather.12 = bf16[128,1280]{1,0:T(8,128)(2,1)S(1)} all-gather(bf16[32,1280]{1,0:T(8,128)(2,1)S(1)} %add_convert_fusion.5), channel_id=1, replica_groups=mesh['section'=4,'batch'=2,'tile'=4] {'tile'}, dimensions={0}, use_global_device_ids=true | all-gather | bytes 409600 | tf_op jit(solution)/shard_map/while/body/eval_jaxpr/all_gather | solution.py:152
  648.1 19.8 %reduce-scatter.2.cloned.1.call-done = bf16[32,1280]{1,0:T(8,128)(2,1)} async-done(((bf16[128,1280]{1,0:T(8,128)(2,1)}), bf16[32,1280]{1,0:T(8,128)(2,1)}) %reduce-scatter.2.cloned.1.call-update) | async-done | bytes 81936 | tf_op jit(solution)/shard_map/while/body/eval_jaxpr/reduce_scatter | solution.py:159
  672.1 38.3 %all-reduce.4.cloned.1.call-done = bf16[4,1,32,1280]{3,2,1,0:T(8,128)(2,1)} async-done(((bf16[4,1,32,1280]{3,2,1,0:T(8,128)(2,1)}), bf16[4,1,32,1280]{3,2,1,0:T(8,128)(2,1)}) %all-reduce.4.cloned.1.call-update) | async-done | bytes 327696 | tf_op jit(solution)/shard_map/psum | solution.py:35
  (464 shorter events, 302.5 us)
Async XLA Ops:
  14.4 58.4 %reduce-scatter.2.cloned.1.call-start = ((), (), s32[]{:S(2)}) async-start(), calls=%async_computation.2 | async-start | bytes 409600 | tf_op jit(solution)/shard_map/while/body/eval_jaxpr/reduce_scatter | solution.py:159
  14.5 15.8 %collective-permute-start = (bf16[1,32,1280]{2,1,0:T(8,128)(2,1)}, bf16[1,32,1280]{2,1,0:T(8,128)(2,1)}, u32[]{:S(2)}, u32[]{:S(2)}) collective-permute-start(bf16[1,32,1280]{2,1,0:T(8,128)(2,1)} %get-tuple-element.768), channel_id=1, source_target_pairs={{0,8},{8,16},{16,24},{24,0},{1,9},{9,17},{17,25},{25,1},{2,10},{10... | collective-permute-start | bytes 245768 | tf_op jit(solution)/shard_map/while/body/eval_jaxpr/ppermute | solution.py:30
  31.3 5.7 collective-permute-start.1
  76.2 56.1 %reduce-scatter.2.cloned.1.call-start = ((), (), s32[]{:S(2)}) async-start(), calls=%async_computation.2 | async-start | bytes 409600 | tf_op jit(solution)/shard_map/while/body/eval_jaxpr/reduce_scatter | solution.py:159
  76.2 14.2 %collective-permute-start = (bf16[1,32,1280]{2,1,0:T(8,128)(2,1)}, bf16[1,32,1280]{2,1,0:T(8,128)(2,1)}, u32[]{:S(2)}, u32[]{:S(2)}) collective-permute-start(bf16[1,32,1280]{2,1,0:T(8,128)(2,1)} %get-tuple-element.768), channel_id=1, source_target_pairs={{0,8},{8,16},{16,24},{24,0},{1,9},{9,17},{17,25},{25,1},{2,10},{10... | collective-permute-start | bytes 245768 | tf_op jit(solution)/shard_map/while/body/eval_jaxpr/ppermute | solution.py:30
  91.4 5.7 collective-permute-start.1
  135.7 56.1 %reduce-scatter.2.cloned.1.call-start = ((), (), s32[]{:S(2)}) async-start(), calls=%async_computation.2 | async-start | bytes 409600 | tf_op jit(solution)/shard_map/while/body/eval_jaxpr/reduce_scatter | solution.py:159
  135.7 14.2 %collective-permute-start = (bf16[1,32,1280]{2,1,0:T(8,128)(2,1)}, bf16[1,32,1280]{2,1,0:T(8,128)(2,1)}, u32[]{:S(2)}, u32[]{:S(2)}) collective-permute-start(bf16[1,32,1280]{2,1,0:T(8,128)(2,1)} %get-tuple-element.768), channel_id=1, source_target_pairs={{0,8},{8,16},{16,24},{24,0},{1,9},{9,17},{17,25},{25,1},{2,10},{10... | collective-permute-start | bytes 245768 | tf_op jit(solution)/shard_map/while/body/eval_jaxpr/ppermute | solution.py:30
  151.0 5.7 collective-permute-start.1
  195.3 56.1 %reduce-scatter.2.cloned.1.call-start = ((), (), s32[]{:S(2)}) async-start(), calls=%async_computation.2 | async-start | bytes 409600 | tf_op jit(solution)/shard_map/while/body/eval_jaxpr/reduce_scatter | solution.py:159
  195.3 14.1 %collective-permute-start = (bf16[1,32,1280]{2,1,0:T(8,128)(2,1)}, bf16[1,32,1280]{2,1,0:T(8,128)(2,1)}, u32[]{:S(2)}, u32[]{:S(2)}) collective-permute-start(bf16[1,32,1280]{2,1,0:T(8,128)(2,1)} %get-tuple-element.768), channel_id=1, source_target_pairs={{0,8},{8,16},{16,24},{24,0},{1,9},{9,17},{17,25},{25,1},{2,10},{10... | collective-permute-start | bytes 245768 | tf_op jit(solution)/shard_map/while/body/eval_jaxpr/ppermute | solution.py:30
  210.5 5.7 collective-permute-start.1
  254.8 56.1 %reduce-scatter.2.cloned.1.call-start = ((), (), s32[]{:S(2)}) async-start(), calls=%async_computation.2 | async-start | bytes 409600 | tf_op jit(solution)/shard_map/while/body/eval_jaxpr/reduce_scatter | solution.py:159
  254.8 14.1 %collective-permute-start = (bf16[1,32,1280]{2,1,0:T(8,128)(2,1)}, bf16[1,32,1280]{2,1,0:T(8,128)(2,1)}, u32[]{:S(2)}, u32[]{:S(2)}) collective-permute-start(bf16[1,32,1280]{2,1,0:T(8,128)(2,1)} %get-tuple-element.768), channel_id=1, source_target_pairs={{0,8},{8,16},{16,24},{24,0},{1,9},{9,17},{17,25},{25,1},{2,10},{10... | collective-permute-start | bytes 245768 | tf_op jit(solution)/shard_map/while/body/eval_jaxpr/ppermute | solution.py:30
  314.3 56.1 %reduce-scatter.2.cloned.1.call-start = ((), (), s32[]{:S(2)}) async-start(), calls=%async_computation.2 | async-start | bytes 409600 | tf_op jit(solution)/shard_map/while/body/eval_jaxpr/reduce_scatter | solution.py:159
  314.3 14.2 %collective-permute-start = (bf16[1,32,1280]{2,1,0:T(8,128)(2,1)}, bf16[1,32,1280]{2,1,0:T(8,128)(2,1)}, u32[]{:S(2)}, u32[]{:S(2)}) collective-permute-start(bf16[1,32,1280]{2,1,0:T(8,128)(2,1)} %get-tuple-element.768), channel_id=1, source_target_pairs={{0,8},{8,16},{16,24},{24,0},{1,9},{9,17},{17,25},{25,1},{2,10},{10... | collective-permute-start | bytes 245768 | tf_op jit(solution)/shard_map/while/body/eval_jaxpr/ppermute | solution.py:30
  329.5 5.7 collective-permute-start.1
  373.8 56.1 %reduce-scatter.2.cloned.1.call-start = ((), (), s32[]{:S(2)}) async-start(), calls=%async_computation.2 | async-start | bytes 409600 | tf_op jit(solution)/shard_map/while/body/eval_jaxpr/reduce_scatter | solution.py:159
  373.8 14.1 %collective-permute-start = (bf16[1,32,1280]{2,1,0:T(8,128)(2,1)}, bf16[1,32,1280]{2,1,0:T(8,128)(2,1)}, u32[]{:S(2)}, u32[]{:S(2)}) collective-permute-start(bf16[1,32,1280]{2,1,0:T(8,128)(2,1)} %get-tuple-element.768), channel_id=1, source_target_pairs={{0,8},{8,16},{16,24},{24,0},{1,9},{9,17},{17,25},{25,1},{2,10},{10... | collective-permute-start | bytes 245768 | tf_op jit(solution)/shard_map/while/body/eval_jaxpr/ppermute | solution.py:30
  389.0 5.7 collective-permute-start.1
  433.3 56.1 %reduce-scatter.2.cloned.1.call-start = ((), (), s32[]{:S(2)}) async-start(), calls=%async_computation.2 | async-start | bytes 409600 | tf_op jit(solution)/shard_map/while/body/eval_jaxpr/reduce_scatter | solution.py:159
  433.3 14.2 %collective-permute-start = (bf16[1,32,1280]{2,1,0:T(8,128)(2,1)}, bf16[1,32,1280]{2,1,0:T(8,128)(2,1)}, u32[]{:S(2)}, u32[]{:S(2)}) collective-permute-start(bf16[1,32,1280]{2,1,0:T(8,128)(2,1)} %get-tuple-element.768), channel_id=1, source_target_pairs={{0,8},{8,16},{16,24},{24,0},{1,9},{9,17},{17,25},{25,1},{2,10},{10... | collective-permute-start | bytes 245768 | tf_op jit(solution)/shard_map/while/body/eval_jaxpr/ppermute | solution.py:30
  448.5 5.7 collective-permute-start.1
  492.8 56.1 %reduce-scatter.2.cloned.1.call-start = ((), (), s32[]{:S(2)}) async-start(), calls=%async_computation.2 | async-start | bytes 409600 | tf_op jit(solution)/shard_map/while/body/eval_jaxpr/reduce_scatter | solution.py:159
  492.8 14.1 %collective-permute-start = (bf16[1,32,1280]{2,1,0:T(8,128)(2,1)}, bf16[1,32,1280]{2,1,0:T(8,128)(2,1)}, u32[]{:S(2)}, u32[]{:S(2)}) collective-permute-start(bf16[1,32,1280]{2,1,0:T(8,128)(2,1)} %get-tuple-element.768), channel_id=1, source_target_pairs={{0,8},{8,16},{16,24},{24,0},{1,9},{9,17},{17,25},{25,1},{2,10},{10... | collective-permute-start | bytes 245768 | tf_op jit(solution)/shard_map/while/body/eval_jaxpr/ppermute | solution.py:30
  552.3 56.1 %reduce-scatter.2.cloned.1.call-start = ((), (), s32[]{:S(2)}) async-start(), calls=%async_computation.2 | async-start | bytes 409600 | tf_op jit(solution)/shard_map/while/body/eval_jaxpr/reduce_scatter | solution.py:159
  552.3 14.2 %collective-permute-start = (bf16[1,32,1280]{2,1,0:T(8,128)(2,1)}, bf16[1,32,1280]{2,1,0:T(8,128)(2,1)}, u32[]{:S(2)}, u32[]{:S(2)}) collective-permute-start(bf16[1,32,1280]{2,1,0:T(8,128)(2,1)} %get-tuple-element.768), channel_id=1, source_target_pairs={{0,8},{8,16},{16,24},{24,0},{1,9},{9,17},{17,25},{25,1},{2,10},{10... | collective-permute-start | bytes 245768 | tf_op jit(solution)/shard_map/while/body/eval_jaxpr/ppermute | solution.py:30
  567.6 5.7 collective-permute-start.1
  611.8 56.1 %reduce-scatter.2.cloned.1.call-start = ((), (), s32[]{:S(2)}) async-start(), calls=%async_computation.2 | async-start | bytes 409600 | tf_op jit(solution)/shard_map/while/body/eval_jaxpr/reduce_scatter | solution.py:159
  611.8 14.1 %collective-permute-start = (bf16[1,32,1280]{2,1,0:T(8,128)(2,1)}, bf16[1,32,1280]{2,1,0:T(8,128)(2,1)}, u32[]{:S(2)}, u32[]{:S(2)}) collective-permute-start(bf16[1,32,1280]{2,1,0:T(8,128)(2,1)} %get-tuple-element.768), channel_id=1, source_target_pairs={{0,8},{8,16},{16,24},{24,0},{1,9},{9,17},{17,25},{25,1},{2,10},{10... | collective-permute-start | bytes 245768 | tf_op jit(solution)/shard_map/while/body/eval_jaxpr/ppermute | solution.py:30
  627.1 5.7 collective-permute-start.1
  671.3 39.1 %all-reduce.4.cloned.1.call-start = ((), (), s32[]{:S(2)}) async-start(), calls=%async_computation.1 | async-start | bytes 655360 | tf_op jit(solution)/shard_map/psum | solution.py:35
  (52 other events, 695.1 us)
Sparse Core Ops, SparseCore 0:
  52.4 20.4 reduce-scatter.1
  111.9 20.3 reduce-scatter.1
  171.5 20.2 reduce-scatter.1
  231.0 20.2 reduce-scatter.1
  290.5 20.2 reduce-scatter.1
  350.0 20.2 reduce-scatter.1
  409.6 20.2 reduce-scatter.1
  469.1 20.3 reduce-scatter.1
  528.6 20.2 reduce-scatter.1
  588.1 20.2 reduce-scatter.1
  647.6 20.2 reduce-scatter.1
Sparse Core Ops, SparseCore 1:
  674.1 36.2 all-reduce.3
where the time goes:
time: 725 us; the launch traced here: 719 us
  waiting for transfers between devices  256 us (35%)
  other arithmetic  102 us (14%)
  matrix products  85.6 us (12%)
  blocking collectives  83.5 us (12%)
  local copies, waits for them, and re-layouts  73.6 us (10%)
  starting transfers between devices  65.6 us (9%)
  loops' own time  38.1 us (5%)
  between operations  14.6 us (2%)
    reduce_scatter x11, waiting for transfers between devices, section_heads(): lax.psum_scatter(jnp.dot(attended, out_local, preferred_element_type=jnp....  218 us
    all_gather x11, blocking collectives, section_heads(): normed_all = lax.all_gather(normed, 'tile', axis=0, tiled=True)  83.5 us
    psum x1, waiting for transfers between devices, spread_2(): return lax.psum(jnp.where(mine, shard, jnp.zeros_like(shard)), axis)  38.3 us
    another operation x1, loops' own time, per_device(): final_state = lax.fori_loop(0, tick_total, advance, initial_latent)  38.1 us
    ppermute x11, starting transfers between devices, extended(): lax.ppermute(tail, axis, [(i, (i + 1) % count) for i in range(ends)])  33.4 us
    slice x33, local copies, waits for them, and re-layouts, section_heads(): values_all = jnp.concatenate([projected[:, 2], prompt_pair[:, 1]], axis=0)  31.8 us
    dot_general x11, matrix products, section_heads(): jnp.dot(attended, out_local, preferred_element_type=jnp.float32)  24.9 us
    reduce_sum x22, other arithmetic, pick_integer(): return jnp.sum(jnp.where(hits, int_table, jnp.zeros_like(int_table)))  21.5 us
  transfers between devices with their start and end apart: 45, of which 12 were waited for; matrix products, arithmetic and copies ran while one was open for 17% of the time, Pallas kernels for 0%

commit v1 on v0

v1 whole, which is shorter than its diff:
```python
import functools
import math

import jax
import jax.numpy as jnp
from jax import lax
from jax.experimental import pallas as pl
from jax.experimental.pallas import tpu as pltpu
from jax.sharding import PartitionSpec as P

HEADS = 20
LANES = 128
MESH = pl.DeviceIdType.MESH


def noise_plan():
    positions = jnp.arange(1000, dtype=jnp.float32)
    low_root = math.sqrt(0.00085)
    high_root = math.sqrt(0.012)
    roots = low_root + (high_root - low_root) * positions / 999.0
    return jnp.exp(jnp.cumsum(jnp.log(1.0 - roots * roots)))


def time_features(timesteps, half_count):
    exponents = jnp.arange(half_count, dtype=jnp.float32) / half_count
    freq_row = jnp.exp(-math.log(10000.0) * exponents)
    angles = timesteps.astype(jnp.float32)[:, None] * freq_row[None, :]
    return jnp.concatenate([jnp.cos(angles), jnp.sin(angles)], axis=1).astype(jnp.bfloat16)


def pick_scalar(alpha_table, position):
    hits = jnp.arange(alpha_table.shape[0], dtype=jnp.int32) == position
    return jnp.sum(jnp.where(hits, alpha_table, jnp.zeros_like(alpha_table)))


def chain_kernel(
    dims,
    coef_ref,
    x0_ref,
    noise_ref,
    temb_ref,
    conv_ref,
    gain_ref,
    bias_ref,
    qkv_ref,
    pkv_ref,
    outw_ref,
    out_ref,
    xin,
    xsend,
    psend,
    precv,
    mixed,
    mixed_own,
    normed,
    proj,
    osend,
    oland,
    x_recv,
    x_send,
    x_fwd,
    p_recv,
    p_send,
    o_recv,
    o_send,
):
    S, T, G, K, M, C, keys_prompt, local_heads, head_width = dims
    n, W = x0_ref.shape[1], x0_ref.shape[2]
    N = T * n
    Q = K * M
    J = T // G
    Hp = outw_ref.shape[0]
    Ws = out_ref.shape[2]
    s = lax.axis_index("section")
    t = lax.axis_index("tile")
    last = s == S - 1
    after = lax.rem(s + 1, S)
    partner = t + 1 - 2 * lax.rem(t, 2)

    barrier = pltpu.get_barrier_semaphore()
    for ds in range(S):
        for dt in range(T):
            if ds or dt:
                pl.semaphore_signal(
                    barrier,
                    inc=1,
                    device_id={"section": lax.rem(s + ds, S), "tile": lax.rem(t + dt, T)},
                    device_id_type=MESH,
                )
    pl.semaphore_wait(barrier, S * T - 1)

    def kin(tile, j):
        return lax.rem(tile + G * j, T)

    def x_copy(src, q, j):
        return pltpu.make_async_remote_copy(
            src_ref=src,
            dst_ref=xin.at[q, t],
            send_sem=x_send.at[q, j],
            recv_sem=x_recv.at[q, t],
            device_id={"section": after, "tile": kin(t, j)},
            device_id_type=MESH,
        )

    def x_relay(q, j):
        row = kin(t, j)
        return pltpu.make_async_remote_copy(
            src_ref=xin.at[q, row],
            dst_ref=xin.at[q, row],
            send_sem=x_fwd.at[q, j],
            recv_sem=x_recv.at[q, row],
            device_id={"section": s, "tile": partner},
            device_id_type=MESH,
        )

    def x_arrived(q, row):
        pltpu.make_async_copy(xin.at[q, row], xin.at[q, row], x_recv.at[q, row]).wait()

    def p_copy(q, d):
        other = lax.rem(t + d, T)
        return pltpu.make_async_remote_copy(
            src_ref=psend.at[q, other],
            dst_ref=precv.at[q, d - 1],
            send_sem=p_send.at[q, d - 1],
            recv_sem=p_recv.at[q, d - 1],
            device_id={"section": s, "tile": other},
            device_id_type=MESH,
        )

    def o_copy(i, d):
        other = lax.rem(s + d, S)
        return pltpu.make_async_remote_copy(
            src_ref=osend.at[i, other],
            dst_ref=oland.at[i],
            send_sem=o_send.at[i, d - 1],
            recv_sem=o_recv.at[i],
            device_id={"section": other, "tile": t},
            device_id_type=MESH,
        )

    @pl.when(last)
    def _():
        for i in range(M):
            for j in range(J):
                x_copy(x0_ref.at[i], i, j).start()

    column = lax.rem(lax.broadcasted_iota(jnp.int32, (N, LANES), 0), C)
    at_left = column == 0
    at_right = column == C - 1

    def compute(q, i, level):
        for j in range(J):
            x_arrived(q, kin(t, j))
            if G > 1:
                x_relay(q, j).start()
        if G > 1:
            for j in range(J):
                x_arrived(q, kin(partner, j))
        total = jnp.zeros((N, LANES), jnp.float32)
        for c in range(W // LANES):
            sl = slice(c * LANES, (c + 1) * LANES)
            x = xin[q, :, :, sl].reshape(N, LANES).astype(jnp.float32)
            x = (x + temb_ref[level, :, sl]).astype(jnp.bfloat16).astype(jnp.float32)
            left = jnp.where(at_left, 0.0, pltpu.roll(x, 1, 0))
            right = jnp.where(at_right, 0.0, pltpu.roll(x, N - 1, 0))
            taps = []
            for a in range(3):
                taps.append(
                    conv_ref[3 * a : 3 * a + 1, sl] * left
                    + conv_ref[3 * a + 1 : 3 * a + 2, sl] * x
                    + conv_ref[3 * a + 2 : 3 * a + 3, sl] * right
                )
            edge = jnp.zeros((C, LANES), jnp.float32)
            value = (
                x
                + jnp.concatenate([edge, taps[0][: N - C]], axis=0)
                + taps[1]
                + jnp.concatenate([taps[2][C:], edge], axis=0)
            )
            mixed[:, :, sl] = value.reshape(T, n, LANES)
            total = total + value
        centre = jnp.sum(total, axis=1, keepdims=True) / W
        total = jnp.zeros((N, LANES), jnp.float32)
        for c in range(W // LANES):
            sl = slice(c * LANES, (c + 1) * LANES)
            delta = mixed[:, :, sl].reshape(N, LANES) - centre
            total = total + delta * delta
        scale = lax.rsqrt(jnp.sum(total, axis=1, keepdims=True) / W + 1e-05)
        for c in range(W // LANES):
            sl = slice(c * LANES, (c + 1) * LANES)
            delta = mixed[:, :, sl].reshape(N, LANES) - centre
            normed[:, sl] = (delta * scale * gain_ref[:, sl] + bias_ref[:, sl]).astype(
                jnp.bfloat16
            )
        mixed_own[i] = mixed[t]
        proj[...] = jnp.dot(
            normed[...], qkv_ref[...], preferred_element_type=jnp.float32
        ).astype(jnp.bfloat16)
        per_block = LANES // head_width
        key_total = N + pkv_ref.shape[2]
        blocks = []
        for b in range(Hp // LANES):
            sl = slice(b * LANES, (b + 1) * LANES)
            heads_here = min(per_block, local_heads - b * per_block)
            query = proj[:, sl]
            keys = jnp.concatenate([proj[:, Hp + b * LANES : Hp + (b + 1) * LANES], pkv_ref[i, 0, :, sl]], axis=0)
            values = jnp.concatenate(
                [proj[:, 2 * Hp + b * LANES : 2 * Hp + (b + 1) * LANES], pkv_ref[i, 1, :, sl]], axis=0
            )
            lane = lax.broadcasted_iota(jnp.int32, (N, LANES), 1) // head_width
            zero = jnp.zeros_like(query)
            stacked = jnp.concatenate(
                [jnp.where(lane == h, query, zero) for h in range(heads_here)], axis=0
            )
            scores = lax.dot_general(
                stacked, keys, (((1,), (1,)), ((), ())), preferred_element_type=jnp.float32
            ) * (1.0 / math.sqrt(head_width))
            real = lax.broadcasted_iota(jnp.int32, scores.shape, 1) < N + keys_prompt
            powers = jnp.where(real, jnp.exp(scores), 0.0)
            soft = (powers * (1.0 / jnp.sum(powers, axis=1, keepdims=True))).astype(jnp.bfloat16)
            got = jnp.dot(soft, values, preferred_element_type=jnp.float32)
            merged = got[:N]
            for h in range(1, heads_here):
                merged = jnp.where(lane == h, got[h * N : (h + 1) * N], merged)
            blocks.append(merged.astype(jnp.bfloat16))
        attended = jnp.concatenate(blocks, axis=1)
        psend[q] = (
            jnp.dot(attended, outw_ref[...], preferred_element_type=jnp.float32)
            .astype(jnp.bfloat16)
            .reshape(T, n, W)
        )
        for d in range(1, T):
            p_copy(q, d).start()

    def finish(q, i, level):
        for d in range(1, T):
            p_copy(q, d).wait_recv()
        update = psend[q, t].astype(jnp.float32)
        for d in range(1, T):
            update = update + precv[q, d - 1].astype(jnp.float32)
        x = (mixed_own[i] + update).astype(jnp.bfloat16)
        final = jnp.logical_and(last, level == K - 1)

        @pl.when(jnp.logical_not(last))
        def _():
            xsend[q] = x
            for j in range(J):
                x_copy(xsend.at[q], q, j).start()

        if K > 1:

            @pl.when(jnp.logical_and(last, level < K - 1))
            def _():
                fresh = noise_ref[lax.rem(level, K - 1), i].astype(jnp.float32)
                later = lax.rem(level + 1, K)
                onward = lax.rem(q + M, Q)
                xsend[onward] = (
                    coef_ref[2 * later] * x.astype(jnp.float32) + coef_ref[2 * later + 1] * fresh
                ).astype(jnp.bfloat16)
                for j in range(J):
                    x_copy(xsend.at[onward], onward, j).start()

        @pl.when(final)
        def _():
            wide = x.astype(jnp.float32)
            for k in range(S):
                turned = wide if k == 0 else pltpu.roll(wide, W - k * Ws, 1)
                osend[i, k] = turned[:, :Ws].astype(jnp.bfloat16)
            for d in range(1, S):
                o_copy(i, d).start()

    def step(k, carry):
        level = k // (M + 1)
        i = lax.rem(k, M + 1)

        @pl.when(i < M)
        def _():
            here = lax.rem(i, M)
            compute(level * M + here, here, level)

        @pl.when(i > 0)
        def _():
            before = lax.rem(i + M - 1, M)
            finish(level * M + before, before, level)

        return carry

    lax.fori_loop(0, K * (M + 1), step, 0)

    def drain(q, carry):
        for j in range(J):
            x_copy(xsend.at[q], q, j).wait_send()
            if G > 1:
                x_relay(q, j).wait_send()
        for d in range(1, T):
            p_copy(q, d).wait_send()
        return carry

    lax.fori_loop(0, Q, drain, 0)

    @pl.when(last)
    def _():
        for i in range(M):
            out_ref[i] = osend[i, S - 1]
            for d in range(1, S):
                o_copy(i, d).wait_send()

    @pl.when(jnp.logical_not(last))
    def _():
        for i in range(M):
            pltpu.make_async_copy(oland.at[i], oland.at[i], o_recv.at[i]).wait()
            out_ref[i] = oland[i]


def per_device(
    latents,
    prompt_tokens,
    fresh_noise,
    timesteps,
    entry_order,
    timestep_weight,
    conv_kernel,
    norm_gain,
    layer_norm_bias,
    qkv_weight,
    prompt_weight,
    out_weight,
):
    S = lax.axis_size("section")
    T = lax.axis_size("tile")
    M, rows_here, C, W = latents.shape
    n = rows_here * C
    K = timesteps.shape[0]
    Q = K * M
    G = 2 if T % 2 == 0 else 1
    J = T // G
    local_heads = HEADS // T
    head_width = W // HEADS
    H = local_heads * head_width
    Hp = -(-H // LANES) * LANES
    text = prompt_tokens.shape[1]
    text_pad = -(-text // LANES) * LANES
    Ws = W // S

    alpha_table = noise_plan()
    alphas = jnp.stack([pick_scalar(alpha_table, timesteps[k]) for k in range(K)])
    coef = jnp.stack([jnp.sqrt(alphas), jnp.sqrt(1.0 - alphas)], axis=1).reshape(2 * K)
    feature_rows = time_features(timesteps, timestep_weight.shape[1] // 2)
    temb = jnp.dot(feature_rows, timestep_weight[0], preferred_element_type=jnp.float32)

    def ordered(array, index):
        return jnp.concatenate(
            [lax.dynamic_slice_in_dim(array, index[m], 1, 0) for m in range(M)], axis=0
        )

    x0 = ordered(latents, entry_order).reshape(M, n, W)
    noise = fresh_noise.reshape(fresh_noise.shape[0], M, n, W)
    tokens = prompt_tokens.reshape(M * text, prompt_tokens.shape[2])
    pkv = jnp.stack(
        [
            jnp.dot(tokens, prompt_weight[0, :, j], preferred_element_type=jnp.float32)
            .astype(jnp.bfloat16)
            .reshape(M, text, H)
            for j in range(2)
        ],
        axis=1,
    )
    pkv = jnp.pad(pkv, ((0, 0), (0, 0), (0, text_pad - text), (0, Hp - H)))
    pkv = ordered(pkv, entry_order)
    qkv = jnp.concatenate(
        [jnp.pad(qkv_weight[0, :, j], ((0, 0), (0, Hp - H))) for j in range(3)], axis=1
    )
    outw = jnp.pad(out_weight[0], ((0, Hp - H), (0, 0)))

    dims = (S, T, G, K, M, C, text, local_heads, head_width)
    vmem = pl.BlockSpec(memory_space=pltpu.VMEM)
    bf16, f32 = jnp.bfloat16, jnp.float32
    dma = pltpu.SemaphoreType.DMA
    results = pl.pallas_call(
        functools.partial(chain_kernel, dims),
        out_shape=jax.ShapeDtypeStruct((M, n, Ws), bf16),
        in_specs=[pl.BlockSpec(memory_space=pltpu.SMEM)] + [vmem] * 9,
        out_specs=vmem,
        scratch_shapes=[
            pltpu.VMEM((Q, T, n, W), bf16),
            pltpu.VMEM((Q, n, W), bf16),
            pltpu.VMEM((Q, T, n, W), bf16),
            pltpu.VMEM((Q, T - 1, n, W), bf16),
            pltpu.VMEM((T, n, W), f32),
            pltpu.VMEM((M, n, W), f32),
            pltpu.VMEM((T * n, W), bf16),
            pltpu.VMEM((T * n, 3 * Hp), bf16),
            pltpu.VMEM((M, S, n, Ws), bf16),
            pltpu.VMEM((M, n, Ws), bf16),
            dma((Q, T)),
            dma((Q, J)),
            dma((Q, J)),
            dma((Q, T - 1)),
            dma((Q, T - 1)),
            dma((M,)),
            dma((M, S - 1)),
        ],
        compiler_params=pltpu.CompilerParams(
            collective_id=0, has_side_effects=True, vmem_limit_bytes=60 * 1024 * 1024
        ),
    )(
        coef,
        x0,
        noise,
        temb.reshape(K, 1, W),
        conv_kernel[0],
        norm_gain,
        layer_norm_bias,
        qkv,
        pkv,
        outw,
    )
    ids = jnp.arange(M, dtype=jnp.int32)
    place = jnp.sum(
        jnp.where(entry_order[None, :] == ids[:, None], ids[None, :], 0), axis=1
    )
    return ordered(results, place).reshape(M, rows_here, C, Ws)


def solution(mesh):
    placed = (
        P("batch", "tile", None, None),
        P("batch", None, None),
        P(None, "batch", "tile", None, None),
        P(),
        P("batch"),
        P("section", None, None),
        P("section", None, None),
        P("section", None),
        P("section", None),
        P("section", None, None, "tile"),
        P("section", None, None, "tile"),
        P("section", "tile", None),
    )
    return jax.shard_map(
        per_device,
        mesh=mesh,
        in_specs=placed,
        out_specs=P("batch", "tile", None, "section"),
        check_vma=False,
    )
```

time: 725 us -> 202 us (0.28)
  waiting for transfers between devices: 256 us -> 0 us
  Pallas kernels: 0 us -> 151 us
  other arithmetic: 102 us -> 9.99 us
  blocking collectives: 83.5 us -> 0 us
  matrix products: 85.6 us -> 5.3 us
  starting transfers between devices: 65.6 us -> 0 us
  local copies, waits for them, and re-layouts: 73.6 us -> 18.9 us
  loops' own time: 38.1 us -> 0 us
    reduce_scatter x11 -> x0, waiting for transfers between devices: 218 us -> none  [section_heads(): lax.psum_scatter(jnp.dot(attended, out_local, preferred_element_type=jnp....]
    pallas_call x0 -> x1, Pallas kernels: none -> 151 us  [per_device(): pl.pallas_call(functools.partial(chain_kernel, dims), out_shape=jax.Shape...]
    all_gather x11 -> x0, blocking collectives: 83.5 us -> none  [section_heads(): normed_all = lax.all_gather(normed, 'tile', axis=0, tiled=True)]
    dot_general x55 -> x2, matrix products: 84.7 us -> 5.03 us  [per_device(): jnp.dot(tokens, prompt_weight[0, :, j], preferred_element_type=jnp.float32)]
    ppermute x33 -> x0, starting transfers between devices: 65.5 us -> none  [the longest x11 33.4 us: extended(): lax.ppermute(tail, axis, [(i, (i + 1) % count) for i in range(ends)])]
    slice x55 -> x5, local copies, waits for them, and re-layouts: 57.7 us -> 6.52 us  [the longest x1 2.99 us: per_device(): qkv_weight[0, :, j]]
    psum x1 -> x0, waiting for transfers between devices: 38.3 us -> none  [spread_2(): return lax.psum(jnp.where(mine, shard, jnp.zeros_like(shard)), axis)]
    select_n x23 -> x0, other arithmetic: 38.2 us -> none  [the longest x11 19.7 us: advance(): results = jnp.where(placing[:, None, None, None], produced[None], results)]
  transfers between devices with their start and end apart: 45 -> 0, of which waited for: 12 -> 0; matrix products, arithmetic and copies ran while one was open for 17% -> 0% of each run, Pallas kernels for 0% -> 0%
where the time goes in v1:
time: 202 us; the launch traced here: 201 us
  Pallas kernels  151 us (75%)
  local copies, waits for them, and re-layouts  18.9 us (9%)
  between operations  15.3 us (8%)
  other arithmetic  9.99 us (5%)
  matrix products  5.3 us (3%)
    pallas_call x1, Pallas kernels, per_device(): pl.pallas_call(functools.partial(chain_kernel, dims), out_shape=jax.Shape...  151 us
    unnamed x13, local copies, waits for them, and re-layouts  6.55 us
    dot_general x2, matrix products, per_device(): jnp.dot(tokens, prompt_weight[0, :, j], preferred_element_type=jnp.float32)  5.03 us

profile of v1, /device:TPU:0, one launch (start us, length us, event | category | flops | bytes accessed | tf_op | source)
XLA Modules:
  0.0 200.8 jit_solution(18217848488826464978)
XLA Ops:
  0.0 0.3 reduce-window.9
  0.4 0.1 slice_reduce_fusion
  0.6 1.3 fusion.36
  1.9 2.0 select_reduce_fusion.1
  3.9 1.2 subtract_sqrt_fusion
  5.2 0.6 reshape.106.coef_ref
  5.8 1.5 fusion.35
  14.9 1.0 constant_dynamic-slice_fusion.11
  15.9 0.8 maximum_bitcast_fusion.x0_ref
  16.7 0.7 convert_element_type.18
  17.4 0.1 fusion.26
  17.5 0.3 fusion.23
  17.8 0.6 reshape.109.temb_ref
  18.4 1.4 copy.48
  19.8 3.0 %fusion.33 = (bf16[1,1280,1,320]{1,3,2,0:T(8,128)(2,1)}, bf16[1,1280,1,320]{1,3,2,0:T(8,128)(2,1)}, bf16[1,1280,1,320]{1,3,2,0:T(8,128)(2,1)S(1)}) fusion(bf16[1,1280,3,320]{1,3,2,0:T(8,128)(2,1)} %param.21), kind=kLoop, calls=%fused_computation.68 | loop fusion | bytes 4915200 | tf_op jit(solution)/shard_map/slice | solution.py:371
  22.8 0.6 copy.46
  23.4 1.6 copy.45
  25.0 2.2 %copy.44 = bf16[1,1280,1,320]{3,1,2,0:T(8,128)(2,1)} copy(bf16[1,1280,1,320]{1,3,2,0:T(8,128)(2,1)} %get-tuple-element.7) | data formatting | bytes 1638400
  27.2 2.9 %fusion.5.qkv_ref = bf16[1280,1152]{1,0:T(8,128)(2,1)} fusion(bf16[1280,320]{1,0:T(8,128)(2,1)S(1)} %bitcast.51, bf16[1280,320]{1,0:T(8,128)(2,1)S(1)} %bitcast.52, bf16[1280,320]{1,0:T(8,128)(2,1)} %bitcast.53), kind=kLoop, calls=%fused_computation.9 | loop fusion | flops 20643840 | bytes 5406720 | tf_op jit(solution)/shard_map/concatenate | solution.py:370
  30.1 0.7 copy.39
  30.8 0.3 reshape.110
  31.2 2.2 %fusion.20 = bf16[308,320]{1,0:T(8,128)(2,1)S(1)} fusion(bf16[308,2048]{1,0:T(8,128)(2,1)S(1)} %reshape.110, bf16[1,2048,2,320]{1,3,2,0:T(8,128)(2,1)} %param.22), kind=kOutput, calls=%fused_computation.24 | convolution fusion | flops 403800320 | bytes 2769408 | tf_op jit(solution)/shard_map/dot_general | solution.py:361
  33.4 2.9 %fusion.17 = bf16[308,320]{1,0:T(8,128)(2,1)} fusion(bf16[308,2048]{1,0:T(8,128)(2,1)S(1)} %reshape.110, bf16[1,2048,2,320]{1,3,2,0:T(8,128)(2,1)} %param.22), kind=kOutput, calls=%fused_computation.23 | convolution fusion | flops 403800320 | bytes 2769408 | tf_op jit(solution)/shard_map/dot_general | solution.py:361
  36.3 1.1 stack_reshape.6
  37.4 0.1 fusion.25
  37.6 1.0 pad_maximum_fusion.pkv_ref
  38.6 1.0 pad.26.outw_ref
  39.6 151.3 %shard_map.118 = bf16[4,32,320]{2,1,0:T(8,128)(2,1)} custom-call(f32[4]{0:T(128)} %reshape.106.coef_ref, bf16[4,32,1280]{2,1,0:T(8,128)(2,1)} %maximum_bitcast_fusion.x0_ref, bf16[1,4,32,1280]{3,2,1,0:T(8,128)(2,1)} %bitcast.57, f32[2,1,1280]{2,1,0:T(1,128)} %reshape.109.temb_ref, f32[9,1280]{1,0:T(8,128)} %bitcast.59, f32[1,1280]{1,0:T(1,128)} %gain_ref.1, ...), custom_call_target="tpu_custom_call" | custom-call | tf_op jit(solution)/shard_map/pallas_call | solution.py:379
  190.9 0.1 select_reduce_fusion.2
  191.1 0.7 fusion.34
  199.3 0.8 constant_dynamic-slice_fusion.3
  200.1 0.7 maximum_bitcast_fusion.1
  (17 shorter events, 0.5 us)
Async XLA Ops:
  0.0 17.5 %copy-start = (bf16[1,320,1280]{2,1,0:T(8,128)(2,1)S(1)}, bf16[1,320,1280]{2,1,0:T(8,128)(2,1)}, u32[]{:S(2)}) copy-start(bf16[1,320,1280]{2,1,0:T(8,128)(2,1)} %param.17) | copy-start | bytes 2457604
  27.2 2.9 %copy-start.1 = (bf16[4,77,2048]{2,0,1:T(4,128)(2,1)S(1)}, bf16[4,77,2048]{2,0,1:T(4,128)(2,1)}, u32[]{:S(2)}) copy-start(bf16[4,77,2048]{2,0,1:T(4,128)(2,1)} %param.13) | copy-start | bytes 3784708
  36.3 2.3 %copy-start.2 = (bf16[1,320,1280]{2,1,0:T(8,128)(2,1)S(1)}, bf16[1,320,1280]{2,1,0:T(8,128)(2,1)}, u32[]{:S(2)}) copy-start(bf16[1,320,1280]{2,1,0:T(8,128)(2,1)} %param.23) | copy-start | bytes 2457604
  39.6 151.3 %copy-start.3 = (s32[4]{0:T(128)S(1)}, s32[4]{0:T(128)}, u32[]{:S(2)}) copy-start(s32[4]{0:T(128)} %param.16) | copy-start | bytes 52

commit v2 on v1

v2 whole, which is shorter than its diff:
```python
import functools
import math

import jax
import jax.numpy as jnp
from jax import lax
from jax.experimental import pallas as pl
from jax.experimental.pallas import tpu as pltpu
from jax.sharding import PartitionSpec as P

HEADS = 20
LANES = 128
MESH = pl.DeviceIdType.MESH


def noise_plan():
    positions = jnp.arange(1000, dtype=jnp.float32)
    low_root = math.sqrt(0.00085)
    high_root = math.sqrt(0.012)
    roots = low_root + (high_root - low_root) * positions / 999.0
    return jnp.exp(jnp.cumsum(jnp.log(1.0 - roots * roots)))


def time_features(timesteps, half_count):
    exponents = jnp.arange(half_count, dtype=jnp.float32) / half_count
    freq_row = jnp.exp(-math.log(10000.0) * exponents)
    angles = timesteps.astype(jnp.float32)[:, None] * freq_row[None, :]
    return jnp.concatenate([jnp.cos(angles), jnp.sin(angles)], axis=1).astype(jnp.bfloat16)


def chain_kernel(
    dims,
    order_ref,
    steps_ref,
    alpha_ref,
    x0_ref,
    noise_ref,
    temb_ref,
    conv_ref,
    gain_ref,
    bias_ref,
    qkv_ref,
    pkv_ref,
    outw_ref,
    out_ref,
    xin,
    xstart,
    xsend,
    psend,
    precv,
    mixed,
    normed,
    proj,
    osend,
    oland,
    x_recv,
    x_send,
    x_fwd,
    p_recv,
    p_send,
    o_recv,
    o_send,
):
    S, T, G, K, M, C, keys_prompt, local_heads, head_width = dims
    n, W = x0_ref.shape[1], x0_ref.shape[2]
    N = T * n
    Q = K * M
    J = T // G
    P_, CW = xsend.shape[1], xsend.shape[3]
    Hp = outw_ref.shape[0]
    Ws = out_ref.shape[2]
    s = lax.axis_index("section")
    t = lax.axis_index("tile")
    last = s == S - 1
    after = lax.rem(s + 1, S)
    partner = t + 1 - 2 * lax.rem(t, 2)

    barrier = pltpu.get_barrier_semaphore()
    for ds in range(S):
        for dt in range(T):
            if ds or dt:
                pl.semaphore_signal(
                    barrier,
                    inc=1,
                    device_id={"section": lax.rem(s + ds, S), "tile": lax.rem(t + dt, T)},
                    device_id_type=MESH,
                )
    pl.semaphore_wait(barrier, S * T - 1)

    def kin(tile, j):
        return lax.rem(tile + G * j, T)

    def x_copy(src, q, p, j):
        return pltpu.make_async_remote_copy(
            src_ref=src,
            dst_ref=xin.at[q, p, t],
            send_sem=x_send.at[q, p, j],
            recv_sem=x_recv.at[q, p, t],
            device_id={"section": after, "tile": kin(t, j)},
            device_id_type=MESH,
        )

    def x_relay(q, p, j):
        row = kin(t, j)
        return pltpu.make_async_remote_copy(
            src_ref=xin.at[q, p, row],
            dst_ref=xin.at[q, p, row],
            send_sem=x_fwd.at[q, p, j],
            recv_sem=x_recv.at[q, p, row],
            device_id={"section": s, "tile": partner},
            device_id_type=MESH,
        )

    def x_arrived(q, p, row):
        here = xin.at[q, p, row]
        pltpu.make_async_copy(here, here, x_recv.at[q, p, row]).wait()

    def p_copy(q, p, d):
        other = lax.rem(t + d, T)
        return pltpu.make_async_remote_copy(
            src_ref=psend.at[q, p, other],
            dst_ref=precv.at[q, p, d - 1],
            send_sem=p_send.at[q, p, d - 1],
            recv_sem=p_recv.at[q, p, d - 1],
            device_id={"section": s, "tile": other},
            device_id_type=MESH,
        )

    def o_copy(i, d):
        other = lax.rem(s + d, S)
        return pltpu.make_async_remote_copy(
            src_ref=osend.at[i, other],
            dst_ref=oland.at[i],
            send_sem=o_send.at[i, d - 1],
            recv_sem=o_recv.at[i],
            device_id={"section": other, "tile": t},
            device_id_type=MESH,
        )

    @pl.when(last)
    def _():
        for i in range(M):
            row = x0_ref[order_ref[i]]
            for p in range(P_):
                xstart[i, p] = row[:, p * CW : (p + 1) * CW]
            for p in range(P_):
                for j in range(J):
                    x_copy(xstart.at[i, p], i, p, j).start()

    column = lax.rem(lax.broadcasted_iota(jnp.int32, (N, LANES), 0), C)
    at_left = column == 0
    at_right = column == C - 1

    def land(q, p):
        for j in range(J):
            x_arrived(q, p, kin(t, j))
            if G > 1:
                x_relay(q, p, j).start()

    def compute(q, i, level):
        land(q, 0)
        total = jnp.zeros((N, LANES), jnp.float32)
        for p in range(P_):
            if p + 1 < P_:
                land(q, p + 1)
            if G > 1:
                for j in range(J):
                    x_arrived(q, p, kin(partner, j))
            for c in range(CW // LANES):
                sl = slice(p * CW + c * LANES, p * CW + (c + 1) * LANES)
                x = xin[q, p, :, :, c * LANES : (c + 1) * LANES]
                x = x.reshape(N, LANES).astype(jnp.float32)
                x = (x + temb_ref[level, :, sl]).astype(jnp.bfloat16).astype(jnp.float32)
                left = jnp.where(at_left, 0.0, pltpu.roll(x, 1, 0))
                right = jnp.where(at_right, 0.0, pltpu.roll(x, N - 1, 0))
                taps = []
                for a in range(3):
                    taps.append(
                        conv_ref[3 * a : 3 * a + 1, sl] * left
                        + conv_ref[3 * a + 1 : 3 * a + 2, sl] * x
                        + conv_ref[3 * a + 2 : 3 * a + 3, sl] * right
                    )
                edge = jnp.zeros((C, LANES), jnp.float32)
                value = (
                    x
                    + jnp.concatenate([edge, taps[0][: N - C]], axis=0)
                    + taps[1]
                    + jnp.concatenate([taps[2][C:], edge], axis=0)
                )
                mixed[:, :, sl] = value.reshape(T, n, LANES)
                total = total + value
        centre = jnp.sum(total, axis=1, keepdims=True) / W
        total = jnp.zeros((N, LANES), jnp.float32)
        for c in range(W // LANES):
            sl = slice(c * LANES, (c + 1) * LANES)
            delta = mixed[:, :, sl].reshape(N, LANES) - centre
            total = total + delta * delta
        scale = lax.rsqrt(jnp.sum(total, axis=1, keepdims=True) / W + 1e-05)
        for c in range(W // LANES):
            sl = slice(c * LANES, (c + 1) * LANES)
            delta = mixed[:, :, sl].reshape(N, LANES) - centre
            normed[:, sl] = (delta * scale * gain_ref[:, sl] + bias_ref[:, sl]).astype(
                jnp.bfloat16
            )
        proj[...] = jnp.dot(
            normed[...], qkv_ref[...], preferred_element_type=jnp.float32
        ).astype(jnp.bfloat16)
        per_block = LANES // head_width
        latent = order_ref[i]
        blocks = []
        for b in range(Hp // LANES):
            sl = slice(b * LANES, (b + 1) * LANES)
            heads_here = min(per_block, local_heads - b * per_block)
            query = proj[:, sl]
            keys = jnp.concatenate(
                [proj[:, Hp + b * LANES : Hp + (b + 1) * LANES], pkv_ref[latent, 0, :, sl]], axis=0
            )
            values = jnp.concatenate(
                [proj[:, 2 * Hp + b * LANES : 2 * Hp + (b + 1) * LANES], pkv_ref[latent, 1, :, sl]],
                axis=0,
            )
            lane = lax.broadcasted_iota(jnp.int32, (N, LANES), 1) // head_width
            zero = jnp.zeros_like(query)
            stacked = jnp.concatenate(
                [jnp.where(lane == h, query, zero) for h in range(heads_here)], axis=0
            )
            scores = lax.dot_general(
                stacked, keys, (((1,), (1,)), ((), ())), preferred_element_type=jnp.float32
            ) * (1.0 / math.sqrt(head_width))
            real = lax.broadcasted_iota(jnp.int32, scores.shape, 1) < N + keys_prompt
            powers = jnp.where(real, jnp.exp(scores), 0.0)
            soft = (powers * (1.0 / jnp.sum(powers, axis=1, keepdims=True))).astype(jnp.bfloat16)
            got = jnp.dot(soft, values, preferred_element_type=jnp.float32)
            merged = got[:N]
            for h in range(1, heads_here):
                merged = jnp.where(lane == h, got[h * N : (h + 1) * N], merged)
            blocks.append(merged.astype(jnp.bfloat16))
        attended = jnp.concatenate(blocks, axis=1)
        for p in range(P_):
            psend[q, p] = (
                jnp.dot(
                    attended,
                    outw_ref[:, p * CW : (p + 1) * CW],
                    preferred_element_type=jnp.float32,
                )
                .astype(jnp.bfloat16)
                .reshape(T, n, CW)
            )
            for d in range(1, T):
                p_copy(q, p, d).start()

    def finish(q, i, level):
        parts = []
        for p in range(P_):
            for d in range(1, T):
                p_copy(q, p, d).wait_recv()
            update = psend[q, p, t].astype(jnp.float32)
            for d in range(1, T):
                update = update + precv[q, p, d - 1].astype(jnp.float32)
            x = (mixed[t, :, p * CW : (p + 1) * CW] + update).astype(jnp.bfloat16)
            parts.append(x)

            @pl.when(jnp.logical_not(last))
            def _():
                xsend[q, p] = x
                for j in range(J):
                    x_copy(xsend.at[q, p], q, p, j).start()

            if K > 1:

                @pl.when(jnp.logical_and(last, level < K - 1))
                def _():
                    later = lax.rem(level + 1, K)
                    onward = lax.rem(q + M, Q)
                    spot = lax.broadcasted_iota(
                        jnp.int32, alpha_ref.shape, 0
                    ) * LANES + lax.broadcasted_iota(jnp.int32, alpha_ref.shape, 1)
                    alpha = jnp.where(spot == steps_ref[later], alpha_ref[...], 0.0)
                    alpha = jnp.sum(jnp.sum(alpha, axis=1, keepdims=True), axis=0, keepdims=True)
                    fresh = noise_ref[lax.rem(level, K - 1), i, :, p * CW : (p + 1) * CW]
                    xsend[onward, p] = (
                        jnp.sqrt(alpha) * x.astype(jnp.float32)
                        + jnp.sqrt(1.0 - alpha) * fresh.astype(jnp.float32)
                    ).astype(jnp.bfloat16)
                    for j in range(J):
                        x_copy(xsend.at[onward, p], onward, p, j).start()

        @pl.when(jnp.logical_and(last, level == K - 1))
        def _():
            wide = jnp.concatenate(parts, axis=1).astype(jnp.float32)
            for k in range(S):
                turned = wide if k == 0 else pltpu.roll(wide, W - k * Ws, 1)
                piece = turned[:, :Ws].astype(jnp.bfloat16)
                if k < S - 1:
                    osend[i, k] = piece
                else:
                    oland[i] = piece
            for d in range(1, S):
                o_copy(i, d).start()

    def step(q, carry):
        level = q // M
        i = lax.rem(q, M)
        compute(q, i, level)
        finish(q, i, level)
        return carry

    lax.fori_loop(0, Q, step, 0)

    def drain(q, carry):
        for p in range(P_):
            for j in range(J):
                x_copy(xsend.at[q, p], q, p, j).wait_send()
                if G > 1:
                    x_relay(q, p, j).wait_send()
            for d in range(1, T):
                p_copy(q, p, d).wait_send()
        return carry

    lax.fori_loop(0, Q, drain, 0)

    @pl.when(last)
    def _():
        for i in range(M):
            for d in range(1, S):
                o_copy(i, d).wait_send()

    @pl.when(jnp.logical_not(last))
    def _():
        for i in range(M):
            pltpu.make_async_copy(oland.at[i], oland.at[i], o_recv.at[i]).wait()

    for m in range(M):
        entry = 0
        for i in range(M):
            entry = jnp.where(order_ref[i] == m, i, entry)
        out_ref[m] = oland[entry]


def per_device(
    latents,
    prompt_tokens,
    fresh_noise,
    timesteps,
    entry_order,
    timestep_weight,
    conv_kernel,
    norm_gain,
    layer_norm_bias,
    qkv_weight,
    prompt_weight,
    out_weight,
):
    S = lax.axis_size("section")
    T = lax.axis_size("tile")
    M, rows_here, C, W = latents.shape
    n = rows_here * C
    K = timesteps.shape[0]
    Q = K * M
    G = 2 if T % 2 == 0 else 1
    J = T // G
    local_heads = HEADS // T
    head_width = W // HEADS
    H = local_heads * head_width
    Hp = -(-H // LANES) * LANES
    text = prompt_tokens.shape[1]
    text_pad = -(-text // LANES) * LANES
    Ws = W // S
    CW = 2 * LANES if W % (2 * LANES) == 0 else LANES
    pieces = W // CW

    alpha_table = noise_plan()
    alpha_rows = -(-alpha_table.shape[0] // (8 * LANES)) * 8
    alpha_table = jnp.pad(alpha_table, (0, alpha_rows * LANES - alpha_table.shape[0]))
    feature_rows = time_features(timesteps, timestep_weight.shape[1] // 2)
    temb = jnp.dot(feature_rows, timestep_weight[0], preferred_element_type=jnp.float32)

    x0 = latents.reshape(M, n, W)
    noise = fresh_noise.reshape(fresh_noise.shape[0], M, n, W)
    tokens = prompt_tokens.reshape(M * text, prompt_tokens.shape[2])
    pkv = jnp.stack(
        [
            jnp.dot(tokens, prompt_weight[0, :, j], preferred_element_type=jnp.float32)
            .astype(jnp.bfloat16)
            .reshape(M, text, H)
            for j in range(2)
        ],
        axis=1,
    )
    pkv = jnp.pad(pkv, ((0, 0), (0, 0), (0, text_pad - text), (0, Hp - H)))
    qkv = jnp.concatenate(
        [jnp.pad(qkv_weight[0, :, j], ((0, 0), (0, Hp - H))) for j in range(3)], axis=1
    )
    outw = jnp.pad(out_weight[0], ((0, Hp - H), (0, 0)))

    dims = (S, T, G, K, M, C, text, local_heads, head_width)
    vmem = pl.BlockSpec(memory_space=pltpu.VMEM)
    bf16, f32 = jnp.bfloat16, jnp.float32
    dma = pltpu.SemaphoreType.DMA
    results = pl.pallas_call(
        functools.partial(chain_kernel, dims),
        out_shape=jax.ShapeDtypeStruct((M, n, Ws), bf16),
        in_specs=[pl.BlockSpec(memory_space=pltpu.SMEM)] * 2 + [vmem] * 10,
        out_specs=vmem,
        scratch_shapes=[
            pltpu.VMEM((Q, pieces, T, n, CW), bf16),
            pltpu.VMEM((M, pieces, n, CW), bf16),
            pltpu.VMEM((Q, pieces, n, CW), bf16),
            pltpu.VMEM((Q, pieces, T, n, CW), bf16),
            pltpu.VMEM((Q, pieces, T - 1, n, CW), bf16),
            pltpu.VMEM((T, n, W), f32),
            pltpu.VMEM((T * n, W), bf16),
            pltpu.VMEM((T * n, 3 * Hp), bf16),
            pltpu.VMEM((M, S, n, Ws), bf16),
            pltpu.VMEM((M, n, Ws), bf16),
            dma((Q, pieces, T)),
            dma((Q, pieces, J)),
            dma((Q, pieces, J)),
            dma((Q, pieces, T - 1)),
            dma((Q, pieces, T - 1)),
            dma((M,)),
            dma((M, S - 1)),
        ],
        compiler_params=pltpu.CompilerParams(
            collective_id=0, has_side_effects=True, vmem_limit_bytes=60 * 1024 * 1024
        ),
    )(
        entry_order,
        timesteps,
        alpha_table.reshape(alpha_rows, LANES),
        x0,
        noise,
        temb.reshape(K, 1, W),
        conv_kernel[0],
        norm_gain,
        layer_norm_bias,
        qkv,
        pkv,
        outw,
    )
    return results.reshape(M, rows_here, C, Ws)


def solution(mesh):
    placed = (
        P("batch", "tile", None, None),
        P("batch", None, None),
        P(None, "batch", "tile", None, None),
        P(),
        P("batch"),
        P("section", None, None),
        P("section", None, None),
        P("section", None),
        P("section", None),
        P("section", None, None, "tile"),
        P("section", None, None, "tile"),
        P("section", "tile", None),
    )
    return jax.shard_map(
        per_device,
        mesh=mesh,
        in_specs=placed,
        out_specs=P("batch", "tile", None, "section"),
        check_vma=False,
    )
```

time: 202 us -> 175 us (0.87)
  between operations: 15.3 us -> 0.09 us
  other arithmetic: 9.99 us -> 4.4 us
  local copies, waits for them, and re-layouts: 18.9 us -> 14.3 us
    slice x4 -> x1, local copies, waits for them, and re-layouts: 3.54 us -> 0.07 us  [the longest x2 2.13 us: ordered(): index[m]]
    reduce_sum x2 -> x0, other arithmetic: 2.09 us -> none  [the longest x1 1.97 us: pick_scalar(): return jnp.sum(jnp.where(hits, alpha_table, jnp.zeros_like(alpha_table)))]
    unnamed x13 -> x16, local copies, waits for them, and re-layouts: 6.55 us -> 7.31 us
where the time goes in v2:
time: 175 us
  Pallas kernels  150 us (86%)
  local copies, waits for them, and re-layouts  14.3 us (8%)
  matrix products  5.3 us (3%)
  other arithmetic  4.4 us (3%)
    pallas_call x1, Pallas kernels, per_device(): pl.pallas_call(functools.partial(chain_kernel, dims), out_shape=jax.Shape...  150 us
    unnamed x16, local copies, waits for them, and re-layouts  7.31 us
    dot_general x2, matrix products, per_device(): jnp.dot(tokens, prompt_weight[0, :, j], preferred_element_type=jnp.float32)  5.04 us

profile of v2, /device:TPU:0, one launch (start us, length us, event | category | flops | bytes accessed | tf_op | source)
XLA Modules:
  0.0 174.5 jit_solution(10198157842621176484)
XLA Ops:
  0.0 0.0 copy-start
  0.0 3.1 %fusion.32 = (bf16[1,1280,1,320]{1,3,2,0:T(8,128)(2,1)S(1)}, bf16[1,1280,1,320]{1,3,2,0:T(8,128)(2,1)}, bf16[1,1280,1,320]{1,3,2,0:T(8,128)(2,1)}) fusion(bf16[1,1280,3,320]{1,3,2,0:T(8,128)(2,1)} %param.21), kind=kLoop, calls=%fused_computation.44 | loop fusion | bytes 4915200 | tf_op jit(solution)/shard_map/slice | solution.py:392
  3.1 0.6 copy.25
  3.7 1.6 copy.26
  5.3 2.2 %copy.27 = bf16[1,1280,1,320]{3,1,2,0:T(8,128)(2,1)} copy(bf16[1,1280,1,320]{1,3,2,0:T(8,128)(2,1)} %get-tuple-element.7) | data formatting | bytes 1638400
  7.5 2.9 %fusion.5.qkv_ref = bf16[1280,1152]{1,0:T(8,128)(2,1)} fusion(bf16[1280,320]{1,0:T(8,128)(2,1)} %bitcast.37, bf16[1280,320]{1,0:T(8,128)(2,1)S(1)} %bitcast.36, bf16[1280,320]{1,0:T(8,128)(2,1)S(1)} %bitcast.35), kind=kLoop, calls=%fused_computation.9 | loop fusion | flops 20643840 | bytes 5406720 | tf_op jit(solution)/shard_map/concatenate | solution.py:391
  10.4 0.0 copy-done.1
  10.4 0.7 copy.20
  11.1 0.3 reshape.44
  11.4 2.2 %fusion.17 = bf16[308,320]{1,0:T(8,128)(2,1)S(1)} fusion(bf16[308,2048]{1,0:T(8,128)(2,1)S(1)} %reshape.44, bf16[1,2048,2,320]{1,3,2,0:T(8,128)(2,1)} %param.22), kind=kOutput, calls=%fused_computation.23 | convolution fusion | flops 403800320 | bytes 2769408 | tf_op jit(solution)/shard_map/dot_general | solution.py:383
  13.6 0.1 stack_reshape.6
  13.7 0.0 copy-start.4
  13.7 2.9 %fusion.20 = bf16[308,320]{1,0:T(8,128)(2,1)} fusion(bf16[308,2048]{1,0:T(8,128)(2,1)S(1)} %reshape.44, bf16[1,2048,2,320]{1,3,2,0:T(8,128)(2,1)} %param.22), kind=kOutput, calls=%fused_computation.24 | convolution fusion | flops 403800320 | bytes 2769408 | tf_op jit(solution)/shard_map/dot_general | solution.py:383
  16.6 0.0 copy-start.3
  16.6 1.1 stack_reshape.7
  17.7 1.0 fusion.25.pkv_ref
  18.7 0.3 reduce-window.9
  19.0 0.1 slice.25
  19.1 0.1 slice_reduce_fusion
  19.2 0.1 add_bitcast_fusion
  19.3 0.6 pad_bitcast_fusion.alpha_ref
  19.9 0.0 copy-done.4
  19.9 0.1 fusion.26
  20.0 0.0 copy-done
  20.1 0.3 fusion.23
  20.3 0.6 reshape.43.temb_ref
  20.9 0.0 copy-done.2
  20.9 1.0 pad.31.outw_ref
  21.9 0.0 copy-done.3
  21.9 0.6 copy.29
  22.6 150.4 %shard_map.118 = bf16[4,32,320]{2,1,0:T(8,128)(2,1)} custom-call(s32[4]{0:T(128)} %order_ref.1, s32[2]{0:T(128)} %steps_ref.1, f32[8,128]{1,0:T(8,128)} %pad_bitcast_fusion.alpha_ref, bf16[4,32,1280]{2,1,0:T(8,128)(2,1)} %bitcast.42, bf16[1,4,32,1280]{3,2,1,0:T(8,128)(2,1)} %bitcast.43, f32[2,1,1280]{2,1,0:T(1,128)} %reshape.43.temb_ref, ...), custom_call_target="tpu_custom_call" | custom-call | tf_op jit(solution)/shard_map/pallas_call | solution.py:400
  173.0 1.5 copy.31
  (8 shorter events, 0.1 us)
Async XLA Ops:
  0.0 20.0 %copy-start = (bf16[1,320,1280]{2,1,0:T(8,128)(2,1)S(1)}, bf16[1,320,1280]{2,1,0:T(8,128)(2,1)}, u32[]{:S(2)}) copy-start(bf16[1,320,1280]{2,1,0:T(8,128)(2,1)} %param.17) | copy-start | bytes 2457604
  7.5 2.9 %copy-start.1 = (bf16[4,77,2048]{2,0,1:T(4,128)(2,1)S(1)}, bf16[4,77,2048]{2,0,1:T(4,128)(2,1)}, u32[]{:S(2)}) copy-start(bf16[4,77,2048]{2,0,1:T(4,128)(2,1)} %param.13) | copy-start | bytes 3784708
  13.7 6.2 %copy-start.4 = (s32[2]{0:T(128)S(1)}, s32[2]{0:T(128)}, u32[]{:S(2)}) copy-start(s32[2]{0:T(128)} %steps_ref.1) | copy-start | bytes 28
  16.6 4.3 %copy-start.2 = (bf16[1,320,1280]{2,1,0:T(8,128)(2,1)S(1)}, bf16[1,320,1280]{2,1,0:T(8,128)(2,1)}, u32[]{:S(2)}) copy-start(bf16[1,320,1280]{2,1,0:T(8,128)(2,1)} %param.23) | copy-start | bytes 2457604
  16.6 5.4 %copy-start.3 = (f32[1,9,1280]{2,0,1:T(1,128)S(1)}, f32[1,9,1280]{2,0,1:T(1,128)}, u32[]{:S(2)}) copy-start(f32[1,9,1280]{2,0,1:T(1,128)} %param.18) | copy-start | bytes 138244

commit v3 on v2

--- a/solution.py
+++ b/solution.py
@@ -202,8 +202,11 @@
             normed[:, sl] = (delta * scale * gain_ref[:, sl] + bias_ref[:, sl]).astype(
                 jnp.bfloat16
             )
-        proj[...] = jnp.dot(
-            normed[...], qkv_ref[...], preferred_element_type=jnp.float32
+        proj[...] = lax.dot_general(
+            normed[...],
+            qkv_ref[...],
+            (((1,), (1,)), ((), ())),
+            preferred_element_type=jnp.float32,
         ).astype(jnp.bfloat16)
         per_block = LANES // head_width
         latent = order_ref[i]
@@ -388,9 +391,8 @@
         axis=1,
     )
     pkv = jnp.pad(pkv, ((0, 0), (0, 0), (0, text_pad - text), (0, Hp - H)))
-    qkv = jnp.concatenate(
-        [jnp.pad(qkv_weight[0, :, j], ((0, 0), (0, Hp - H))) for j in range(3)], axis=1
-    )
+    qkv = jnp.transpose(qkv_weight[0], (1, 2, 0))
+    qkv = jnp.pad(qkv, ((0, 0), (0, Hp - H), (0, 0))).reshape(3 * Hp, W)
     outw = jnp.pad(out_weight[0], ((0, Hp - H), (0, 0)))
 
     dims = (S, T, G, K, M, C, text, local_heads, head_width)

time: 175 us -> 181 us (1.034)
  Pallas kernels: 150 us -> 159 us
  local copies, waits for them, and re-layouts: 14.3 us -> 12 us
    pallas_call x1, Pallas kernels: 150 us -> 159 us  [per_device(): pl.pallas_call(functools.partial(chain_kernel, dims), out_shape=jax.Shape...]
    slice x2 -> x1, local copies, waits for them, and re-layouts: 3.14 us -> 0.07 us  [the longest x1 3.06 us: per_device(): qkv_weight[0, :, j]]
    concatenate x1 -> x0, other arithmetic: 2.89 us -> none  [per_device(): jnp.concatenate([jnp.pad(qkv_weight[0, :, j], ((0, 0), (0, Hp - H))) for...]
    unnamed x16 -> x15, local copies, waits for them, and re-layouts: 7.31 us -> 4.73 us
where the time goes in v3:
time: 181 us
  Pallas kernels  159 us (88%)
  local copies, waits for them, and re-layouts  12 us (7%)
  matrix products  6.27 us (3%)
  other arithmetic  3.26 us (2%)
    pallas_call x1, Pallas kernels, per_device(): pl.pallas_call(functools.partial(chain_kernel, dims), out_shape=jax.Shape...  159 us
    dot_general x2, matrix products, per_device(): jnp.dot(tokens, prompt_weight[0, :, j], preferred_element_type=jnp.float32)  6.01 us
    unnamed x15, local copies, waits for them, and re-layouts  4.73 us

profile of v3, /device:TPU:0, one launch (start us, length us, event | category | flops | bytes accessed | tf_op | source)
XLA Modules:
  0.0 180.8 jit_solution(11626468479615558271)
XLA Ops:
  0.0 0.0 copy-start
  0.0 0.0 copy-start.4
  0.0 0.0 copy-start.3
  0.0 0.8 convert_element_type.18
  0.8 0.1 fusion.20
  1.0 0.3 reduce-window.9
  1.3 0.1 slice.16
  1.4 0.1 slice_reduce_fusion
  1.5 0.1 add_bitcast_fusion
  1.6 0.6 pad_bitcast_fusion.alpha_ref
  2.2 0.0 copy-done
  2.2 0.3 fusion.17
  2.4 0.6 reshape.46.temb_ref
  3.0 1.4 copy.20
  4.5 0.0 copy-done.4
  4.5 1.0 pad.23.outw_ref
  5.5 0.0 copy-done.3
  5.5 0.7 copy.14
  6.2 0.3 reshape.48
  6.5 0.0 copy-start.2
  6.6 1.0 copy-done.2
  7.6 0.0 copy-start.5
  7.6 3.0 %fusion.14 = bf16[308,320]{1,0:T(8,128)(2,1)} fusion(bf16[308,2048]{1,0:T(8,128)(2,1)S(1)} %reshape.48, bf16[1,2048,2,320]{1,3,2,0:T(8,128)(2,1)} %param.22), kind=kOutput, calls=%fused_computation.14 | convolution fusion | flops 403800320 | bytes 2769408 | tf_op jit(solution)/shard_map/dot_general | solution.py:386
  10.6 0.0 copy-done.5
  10.6 3.0 %fusion.11 = bf16[308,320]{1,0:T(8,128)(2,1)} fusion(bf16[308,2048]{1,0:T(8,128)(2,1)} %copy-done.2, bf16[1,2048,2,320]{1,3,2,0:T(8,128)(2,1)S(1)} %copy-done.5), kind=kOutput, calls=%fused_computation.13 | convolution fusion | flops 403800320 | bytes 2769408 | tf_op jit(solution)/shard_map/dot_general | solution.py:386
  13.6 1.0 stack_reshape.6
  14.6 1.7 stack_reshape.7
  16.3 1.9 %fusion.19.pkv_ref = bf16[4,2,128,384]{3,2,1,0:T(8,128)(2,1)} fusion(bf16[4,1,77,320]{3,2,1,0:T(8,128)(2,1)} %bitcast.39, bf16[4,1,77,320]{3,2,1,0:T(8,128)(2,1)S(1)} %bitcast.38), kind=kLoop, calls=%fused_computation.17 | loop fusion | flops 4325376 | bytes 1180672 | tf_op jit(solution)/shard_map/stack | solution.py:384
  18.3 0.0 copy-done.1
  18.3 1.8 pad.21
  20.1 159.2 %shard_map.118 = bf16[4,32,320]{2,1,0:T(8,128)(2,1)} custom-call(s32[4]{0:T(128)} %order_ref.1, s32[2]{0:T(128)} %steps_ref.1, f32[8,128]{1,0:T(8,128)} %pad_bitcast_fusion.alpha_ref, bf16[4,32,1280]{2,1,0:T(8,128)(2,1)} %bitcast.42, bf16[1,4,32,1280]{3,2,1,0:T(8,128)(2,1)} %bitcast.43, f32[2,1,1280]{2,1,0:T(1,128)} %reshape.46.temb_ref, ...), custom_call_target="tpu_custom_call" | custom-call | tf_op jit(solution)/shard_map/pallas_call | solution.py:402
  179.2 1.5 copy.22
  (6 shorter events, 0.1 us)
Async XLA Ops:
  0.0 2.2 %copy-start = (bf16[1,320,1280]{2,1,0:T(8,128)(2,1)S(1)}, bf16[1,320,1280]{2,1,0:T(8,128)(2,1)}, u32[]{:S(2)}) copy-start(bf16[1,320,1280]{2,1,0:T(8,128)(2,1)} %param.17) | copy-start | bytes 2457604
  0.0 4.5 %copy-start.4 = (bf16[1,320,1280]{2,1,0:T(8,128)(2,1)S(1)}, bf16[1,320,1280]{2,1,0:T(8,128)(2,1)}, u32[]{:S(2)}) copy-start(bf16[1,320,1280]{2,1,0:T(8,128)(2,1)} %param.23) | copy-start | bytes 2457604
  0.0 5.5 %copy-start.3 = (bf16[4,77,2048]{2,0,1:T(4,128)(2,1)S(1)}, bf16[4,77,2048]{2,0,1:T(4,128)(2,1)}, u32[]{:S(2)}) copy-start(bf16[4,77,2048]{2,0,1:T(4,128)(2,1)} %param.13) | copy-start | bytes 3784708
  6.5 1.0 copy-start.2
  7.6 3.0 %copy-start.5 = (bf16[1,2048,2,320]{1,3,2,0:T(8,128)(2,1)S(1)}, bf16[1,2048,2,320]{1,3,2,0:T(8,128)(2,1)}, u32[]{:S(2)}) copy-start(bf16[1,2048,2,320]{1,3,2,0:T(8,128)(2,1)} %param.22) | copy-start | bytes 7864324
  10.6 7.6 %copy-start.1 = (bf16[1,1280,3,320]{1,3,2,0:T(8,128)(2,1)S(1)}, bf16[1,1280,3,320]{1,3,2,0:T(8,128)(2,1)}, u32[]{:S(2)}) copy-start(bf16[1,1280,3,320]{1,3,2,0:T(8,128)(2,1)} %param.21) | copy-start | bytes 7372804
